TPU v7x, 256 devices: a whole 4x4x8 slice. The times are simulated.
256 devices in a mesh: lev: 2 (over core), wa: 128 (over y, z, x).
Axes of the slice: x: 4, y: 4, z: 8, core: 2. Of those that a mesh axis runs over, the one named last changes fastest.
Arguments:
- spectral: bfloat16 [1280, 1280, 2, 64], P('wa', None, None, 'lev'), parts along dimension 3, may hold values from -0.15625 to 0.15625
- legendre: bfloat16 [1280, 1280, 384], P('wa'), may hold values from -0.15625 to 0.15625
- wavenumber: int32 [1280], P('wa'), may hold values from 0 to 1279, each once
Outputs:
- grid: float32 [768, 2560, 64], P('wa', None, 'lev'), parts along dimension 2
There are 2 independent parts, one for each index of `lev`. A program takes and returns all parts, laid end to end along the dimension named above; an argument that names none is the same for every part. Nothing has to cross between parts.
Inputs may be any that keep to these rules, and one draw needn't show every extreme that they name: wavenumber names every number of 0 to 1279 exactly once; slot k of spectral and legendre belongs to wavenumber[k].
All inputs are finite; a program needn't handle non-finite values.
Results may differ from a plain program's by a relative error of at most 0.0003.
Values sent between devices are 32-bit elements.
A program may use at most 128 MiB of HBM per device.

v0:
```python
import functools
import math

import jax
import jax.numpy as jnp
from jax import lax
from jax.experimental import pallas as pl
from jax.experimental.pallas import tpu as pltpu
from jax.sharding import PartitionSpec as P

NLON = 2560
TILE = 256
LANES = 128
NY, NZ, NX = 4, 8, 4
PLANE = NY * NX
OWNERS = NY * NZ * NX


def cos_sin(turns):
    quarter = jnp.floor(turns * (4.0 / NLON) + 0.5)
    x = (turns - quarter * (NLON // 4)) * (2.0 * math.pi / NLON)
    y = x * x
    s = x * (1.0 + y * (-1 / 6 + y * (1 / 120 + y * (-1 / 5040 + y * (1 / 362880)))))
    c = 1.0 + y * (-1 / 2 + y * (1 / 24 + y * (-1 / 720 + y * (1 / 40320 - y * (1 / 3628800)))))
    which = quarter.astype(jnp.int32) & 3
    odd = (which & 1) == 1
    cos_out = jnp.where(odd, s, c)
    sin_out = jnp.where(odd, c, s)
    cos_out = jnp.where((which == 1) | (which == 2), -cos_out, cos_out)
    sin_out = jnp.where(which >= 2, -sin_out, sin_out)
    return cos_out, sin_out


def transform_kernel(
    chunks, rows,
    wave_smem, spectral_hbm, legendre_hbm,
    out,
    spectral, legendre, staged, send, middle, recv,
    wave_row, wave_mid, wave_all, wave_rows,
    cos_hi, cos_lo, sin_hi, sin_lo, even, odd,
    load_sem, z_send, z_recv, p_send, p_recv, own_sem,
):
    me = lax.axis_index("wa")
    y, z, x = me // (NZ * NX), (me // NX) % NZ, me % NX
    place = y * NX + x
    slots, columns, degrees = spectral.shape
    north = legendre.shape[2]
    levels = columns // 2

    def peer_at(py, pz, px):
        return (py * NZ + pz) * NX + px

    def remote(src, dst, send_sem, recv_sem, peer):
        return pltpu.make_async_remote_copy(
            src_ref=src, dst_ref=dst, send_sem=send_sem, recv_sem=recv_sem,
            device_id={"wa": peer}, device_id_type=pl.DeviceIdType.MESH,
        )

    def each_z(act):
        for d in (4, 3, 5, 2, 6, 1, 7):
            act((z + d) % NZ)

    def each_place(act):
        for d in (5, 10, 15, 2, 8, 7, 13, 1, 4, 3, 12, 6, 9, 11, 14):
            act((y + d // NX) % NY, (x + d % NX) % NX)

    def z_copy(c, to, owner):
        return remote(
            send.at[c, :, to, :, 0:rows, :], middle.at[c, owner, :, :, 0:rows, :],
            z_send.at[c, to], z_recv.at[c, owner], peer_at(y, to, x),
        )

    def z_own(c):
        return pltpu.make_async_copy(
            send.at[c, :, z, :, 0:rows, :], middle.at[c, z, :, :, 0:rows, :], own_sem.at[0, c]
        )

    def p_copy(c, py, px, owner):
        return remote(
            middle.at[c, :, py, px, 0:rows, :], recv.at[c, owner, :, 0:rows, :],
            p_send.at[c, py * NX + px], p_recv.at[c, owner], peer_at(py, z, px),
        )

    def p_own(c):
        return pltpu.make_async_copy(
            middle.at[c, :, y, x, 0:rows, :], recv.at[c, place, :, 0:rows, :], own_sem.at[1, c]
        )

    def wave_z(to, owner):
        return remote(
            wave_row.at[0:1, :], wave_mid.at[owner, 0:1, :],
            z_send.at[chunks, to], z_recv.at[chunks, owner], peer_at(y, to, x),
        )

    wave_z_own = pltpu.make_async_copy(
        wave_row.at[0:1, :], wave_mid.at[z, 0:1, :], own_sem.at[0, chunks]
    )

    def wave_p(py, px, owner):
        return remote(
            wave_mid.at[:, 0:1, :], wave_all.at[owner, :, 0:1, :],
            p_send.at[chunks, py * NX + px], p_recv.at[chunks, owner], peer_at(py, z, px),
        )

    wave_p_own = pltpu.make_async_copy(
        wave_mid.at[:, 0:1, :], wave_all.at[place, :, 0:1, :], own_sem.at[1, chunks]
    )

    def load(slot):
        return (
            pltpu.make_async_copy(spectral_hbm.at[slot], spectral.at[slot], load_sem.at[0, slot]),
            pltpu.make_async_copy(legendre_hbm.at[slot], legendre.at[slot], load_sem.at[1, slot]),
        )

    for slot in range(slots):
        for copy in load(slot):
            copy.start()

    barrier = pltpu.get_barrier_semaphore()

    def greet(peer):
        pl.semaphore_signal(
            barrier, inc=1, device_id={"wa": peer}, device_id_type=pl.DeviceIdType.MESH
        )

    each_z(lambda to: greet(peer_at(y, to, x)))
    each_place(lambda py, px: greet(peer_at(py, z, px)))
    at_slot = lax.broadcasted_iota(jnp.int32, wave_row.shape, 1)
    waves = jnp.zeros(wave_row.shape, jnp.int32)
    for slot in range(slots):
        waves = jnp.where(at_slot == slot, wave_smem[slot], waves)
    wave_row[...] = waves
    staged[...] = jnp.zeros(staged.shape, jnp.float32)
    pl.semaphore_wait(barrier, NZ - 1 + PLANE - 1)
    each_z(lambda to: wave_z(to, z).start())
    wave_z_own.start()

    index = lax.broadcasted_iota(jnp.int32, (1, degrees), 1)

    def sums_of(slot):
        for copy in load(slot):
            copy.wait()
        offset = index - wave_smem[slot]
        keep = jnp.where(offset >= 0, 1.0, 0.0)
        flip = jnp.where((offset & 1) == 0, keep, -keep)
        coeff = spectral[slot]
        both = jnp.concatenate(
            [coeff * keep.astype(coeff.dtype), coeff * flip.astype(coeff.dtype)], 0
        )
        return jnp.dot(both, legendre[slot], preferred_element_type=jnp.float32)

    def synthesize(c, carry):
        first = sums_of(2 * c)
        second = sums_of(2 * c + 1)
        for side in range(2):
            part = slice(side * columns, (side + 1) * columns)
            staged[side, 0:north, :] = jnp.concatenate([first[part], second[part]], 0).T
            for slab in range(OWNERS // 2):
                d = OWNERS - 1 - slab if side else slab
                send[c, d // (NZ * NX), (d // NX) % NZ, d % NX] = staged[
                    side, rows * slab:rows * slab + 8, :
                ]
        each_z(lambda to: z_copy(c, to, z).start())
        z_own(c).start()
        return carry

    lax.fori_loop(0, chunks, synthesize, 0)

    wave_z_own.wait()
    each_z(lambda to: wave_z(to, to).wait_recv())
    each_place(lambda py, px: wave_p(py, px, place).start())
    wave_p_own.start()
    even[...] = jnp.zeros(even.shape, jnp.float32)
    odd[...] = jnp.zeros(odd.shape, jnp.float32)

    wave_p_own.wait()
    each_place(lambda py, px: wave_p(py, px, py * NX + px).wait_recv())
    flat_waves = wave_all.reshape(OWNERS * 8, LANES)
    gathered = flat_waves[pl.ds(0, OWNERS, stride=8), :].astype(jnp.float32)
    for slot in range(slots):
        wave_rows[slot * OWNERS:(slot + 1) * OWNERS, :] = jnp.broadcast_to(
            gathered[:, slot:slot + 1], (OWNERS, LANES)
        )
    position = lax.broadcasted_iota(jnp.int32, (1, LANES), 1).astype(jnp.float32)
    sin_tiles = sin_hi.shape[1] // LANES

    def fill(i, carry):
        at = pl.ds(pl.multiple_of(i * 16, 16), 16)
        waves = wave_rows[at, :]
        weight = jnp.where(waves == 0.0, 1.0, 2.0)
        c, s = cos_sin(waves * position)
        turn_c, turn_s = cos_sin(waves * float(LANES))
        c, s = c * weight, s * weight
        for tile in range(sin_tiles + 1):
            to = slice(tile * LANES, (tile + 1) * LANES)
            top = c.astype(jnp.bfloat16)
            cos_hi[at, to] = top
            cos_lo[at, to] = (c - top.astype(jnp.float32)).astype(jnp.bfloat16)
            if tile < sin_tiles:
                top = s.astype(jnp.bfloat16)
                sin_hi[at, to] = top
                sin_lo[at, to] = (s - top.astype(jnp.float32)).astype(jnp.bfloat16)
                c, s = c * turn_c - s * turn_s, s * turn_c + c * turn_s
        return carry

    south = me // (OWNERS // 2)
    flat = recv.reshape(chunks * OWNERS * 8, LANES)

    def forward(c):
        z_own(c).wait()
        each_z(lambda to: z_copy(c, to, to).wait_recv())
        each_place(lambda py, px: p_copy(c, py, px, place).start())
        p_own(c).start()

    def add_chunk(c):
        p_own(c).wait()
        each_place(lambda py, px: p_copy(c, py, px, py * NX + px).wait_recv())
        parts = [[], []]
        for row in range(rows):
            source = row + south * (rows - 1 - 2 * row)
            turned = flat[pl.ds(c * OWNERS * 8 + source, OWNERS, stride=8), :].T
            for part in range(2):
                parts[part].append(
                    jnp.concatenate(
                        [turned[part * levels:(part + 1) * levels],
                         turned[(2 + part) * levels:(3 + part) * levels]], 1
                    )
                )
        at = pl.ds(pl.multiple_of(c * 2 * OWNERS, 2 * OWNERS), 2 * OWNERS)
        for part, total, high, low in ((0, even, cos_hi, cos_lo), (1, odd, sin_hi, sin_lo)):
            values = jnp.concatenate(parts[part], 0)
            top = values.astype(jnp.bfloat16)
            rest = (values - top.astype(jnp.float32)).astype(jnp.bfloat16)
            table = high[at, :]
            sums = jnp.dot(top, table, preferred_element_type=jnp.float32)
            sums += jnp.dot(rest, table, preferred_element_type=jnp.float32)
            sums += jnp.dot(top, low[at, :], preferred_element_type=jnp.float32)
            total[...] += sums

    forward(0)
    lax.fori_loop(0, wave_rows.shape[0] // 16, fill, 0)

    def later(c, carry):
        @pl.when(c < chunks)
        def _():
            forward(c)

        add_chunk(c - 1)
        return carry

    lax.fori_loop(1, chunks + 1, later, 0)

    r = lax.broadcasted_iota(jnp.int32, (TILE, TILE), 0)
    q = lax.broadcasted_iota(jnp.int32, (TILE, TILE), 1)
    mirror = jnp.where(r + q == TILE, 1.0, 0.0).astype(jnp.bfloat16)
    at_zero = lax.broadcasted_iota(jnp.int32, (1, TILE), 1) == 0
    tiles = odd.shape[1] // TILE
    after = even[:, tiles * TILE:tiles * TILE + 1]
    for tile in range(tiles - 1, -1, -1):
        to = slice(tile * TILE, (tile + 1) * TILE)
        back = slice((2 * tiles - 1 - tile) * TILE, (2 * tiles - tile) * TILE)
        e, o = even[:, to], odd[:, to]
        out[:, :, to] = (e - o).reshape(rows, levels, TILE)
        d = e + o
        top = d.astype(jnp.bfloat16)
        rest = (d - top.astype(jnp.float32)).astype(jnp.bfloat16)
        turned = jnp.dot(top, mirror, preferred_element_type=jnp.float32)
        turned += jnp.dot(rest, mirror, preferred_element_type=jnp.float32)
        out[:, :, back] = jnp.where(at_zero, after, turned).reshape(rows, levels, TILE)
        after = d[:, 0:1]

    each_z(lambda to: wave_z(to, z).wait_send())
    each_place(lambda py, px: wave_p(py, px, place).wait_send())

    def drain(c, carry):
        each_z(lambda to: z_copy(c, to, z).wait_send())
        each_place(lambda py, px: p_copy(c, py, px, place).wait_send())
        return carry

    lax.fori_loop(0, chunks, drain, 0)


def on_device(spectral, legendre, wavenumber):
    slots, degrees, _, levels = spectral.shape
    north = legendre.shape[2]
    rows = 2 * north // OWNERS
    chunks = slots // 2
    coeff = jnp.transpose(spectral, (0, 2, 3, 1)).reshape(slots, 2 * levels, degrees)
    depth = slots * OWNERS
    half = NLON // 2
    f32, bf16, i32 = jnp.float32, jnp.bfloat16, jnp.int32
    grid = pl.pallas_call(
        functools.partial(transform_kernel, chunks, rows),
        out_shape=jax.ShapeDtypeStruct((rows, levels, NLON), f32),
        in_specs=[
            pl.BlockSpec(memory_space=pltpu.SMEM),
            pl.BlockSpec(memory_space=pltpu.HBM),
            pl.BlockSpec(memory_space=pltpu.HBM),
        ],
        out_specs=pl.BlockSpec(memory_space=pltpu.VMEM),
        scratch_shapes=[
            pltpu.VMEM((slots, 2 * levels, degrees), bf16),
            pltpu.VMEM((slots, degrees, north), bf16),
            pltpu.VMEM((2, north + 8, LANES), f32),
            pltpu.VMEM((chunks, NY, NZ, NX, 8, LANES), f32),
            pltpu.VMEM((chunks, NZ, NY, NX, 8, LANES), f32),
            pltpu.VMEM((chunks, PLANE, NZ, 8, LANES), f32),
            pltpu.VMEM((8, LANES), i32),
            pltpu.VMEM((NZ, 8, LANES), i32),
            pltpu.VMEM((PLANE, NZ, 8, LANES), i32),
            pltpu.VMEM((depth, LANES), f32),
            pltpu.VMEM((depth, half + LANES), bf16),
            pltpu.VMEM((depth, half + LANES), bf16),
            pltpu.VMEM((depth, half), bf16),
            pltpu.VMEM((depth, half), bf16),
            pltpu.VMEM((rows * levels, half + LANES), f32),
            pltpu.VMEM((rows * levels, half), f32),
            pltpu.SemaphoreType.DMA((2, slots)),
            pltpu.SemaphoreType.DMA((chunks + 1, NZ)),
            pltpu.SemaphoreType.DMA((chunks + 1, NZ)),
            pltpu.SemaphoreType.DMA((chunks + 1, PLANE)),
            pltpu.SemaphoreType.DMA((chunks + 1, PLANE)),
            pltpu.SemaphoreType.DMA((2, chunks + 1)),
        ],
        compiler_params=pltpu.CompilerParams(
            collective_id=0, has_side_effects=True, vmem_limit_bytes=60 * 2**20,
        ),
    )(wavenumber, coeff, legendre)
    return jnp.transpose(grid, (0, 2, 1))


def solution(mesh):
    return jax.shard_map(
        on_device,
        mesh=mesh,
        in_specs=(P("wa", None, None, "lev"), P("wa", None, None), P("wa")),
        out_specs=P("wa", None, "lev"),
        check_vma=False,
    )
```

profile of v0, /device:TPU:1, one launch (start us, length us, event | category | flops | bytes accessed | tf_op | source)
XLA Modules:
  0.0 73.2 jit_solution(5968944400258025840)
XLA Ops:
  0.0 70.2 %shard_map.37 = f32[6,32,2560]{2,1,0:T(8,128)} custom-call(s32[10]{0:T(128)} %wave_smem.1, bf16[10,64,1280]{2,1,0:T(8,128)(2,1)} %bitcast.5, bf16[10,1280,384]{2,1,0:T(8,128)(2,1)} %legendre_hbm.1), custom_call_target="tpu_custom_call" | custom-call | tf_op jit(solution)/shard_map/pallas_call | solution.py:292
  70.2 3.0 %copy.5 = f32[6,2560,32]{1,2,0:T(8,128)} copy(f32[6,2560,32]{1,2,0:T(8,128)} %bitcast.4) | data formatting | bytes 3932160
where the time goes:
time: 73.3 us; the launch traced here: 73.2 us
  Pallas kernels  70.2 us (96%)
  local copies, waits for them, and re-layouts  2.99 us (4%)
    pallas_call x1, Pallas kernels, on_device(): pl.pallas_call(functools.partial(transform_kernel, chunks, rows), out_sha...  70.2 us
    unnamed x1, local copies, waits for them, and re-layouts  2.99 us

commit v1 on v0

--- a/solution.py
+++ b/solution.py
@@ -32,10 +32,10 @@
 
 
 def transform_kernel(
-    chunks, rows,
+    chunks, line_first, rows,
     wave_smem, spectral_hbm, legendre_hbm,
     out,
-    spectral, legendre, staged, send, middle, recv,
+    spectral, legendre, staged, send, middle, spread, recv,
     wave_row, wave_mid, wave_all, wave_rows,
     cos_hi, cos_lo, sin_hi, sin_lo, even, odd,
     load_sem, z_send, z_recv, p_send, p_recv, own_sem,
@@ -61,30 +61,58 @@
             act((z + d) % NZ)
 
     def each_place(act):
-        for d in (5, 10, 15, 2, 8, 7, 13, 1, 4, 3, 12, 6, 9, 11, 14):
+        for d in (5, 15, 7, 13, 10, 6, 9, 14, 11, 2, 8, 1, 4, 3, 12):
             act((y + d // NX) % NY, (x + d % NX) % NX)
 
     def z_copy(c, to, owner):
+        if c < line_first:
+            src, dst = send.at[c, :, to, :, 0:rows, :], middle.at[c, owner, :, :, 0:rows, :]
+        else:
+            src = spread.at[c - line_first, :, to, 0:rows, :]
+            dst = recv.at[c, :, owner, 0:rows, :]
+        return remote(src, dst, z_send.at[c, to], z_recv.at[c, owner], peer_at(y, to, x))
+
+    def z_own(c):
+        if c < line_first:
+            src, dst = send.at[c, :, z, :, 0:rows, :], middle.at[c, z, :, :, 0:rows, :]
+        else:
+            src = spread.at[c - line_first, :, z, 0:rows, :]
+            dst = recv.at[c, :, z, 0:rows, :]
+        return pltpu.make_async_copy(src, dst, own_sem.at[0, c])
+
+    def p_copy(c, py, px, owner):
+        if c < line_first:
+            src, dst = middle.at[c, :, py, px, 0:rows, :], recv.at[c, owner, :, 0:rows, :]
+        else:
+            src = send.at[c, py, :, px, 0:rows, :]
+            dst = spread.at[c - line_first, owner, :, 0:rows, :]
         return remote(
-            send.at[c, :, to, :, 0:rows, :], middle.at[c, owner, :, :, 0:rows, :],
-            z_send.at[c, to], z_recv.at[c, owner], peer_at(y, to, x),
-        )
-
-    def z_own(c):
-        return pltpu.make_async_copy(
-            send.at[c, :, z, :, 0:rows, :], middle.at[c, z, :, :, 0:rows, :], own_sem.at[0, c]
-        )
-
-    def p_copy(c, py, px, owner):
-        return remote(
-            middle.at[c, :, py, px, 0:rows, :], recv.at[c, owner, :, 0:rows, :],
-            p_send.at[c, py * NX + px], p_recv.at[c, owner], peer_at(py, z, px),
+            src, dst, p_send.at[c, py * NX + px], p_recv.at[c, owner], peer_at(py, z, px)
         )
 
     def p_own(c):
-        return pltpu.make_async_copy(
-            middle.at[c, :, y, x, 0:rows, :], recv.at[c, place, :, 0:rows, :], own_sem.at[1, c]
-        )
+        if c < line_first:
+            src, dst = middle.at[c, :, y, x, 0:rows, :], recv.at[c, place, :, 0:rows, :]
+        else:
+            src = send.at[c, y, :, x, 0:rows, :]
+            dst = spread.at[c - line_first, place, :, 0:rows, :]
+        return pltpu.make_async_copy(src, dst, own_sem.at[1, c])
+
+    def start_z(c):
+        each_z(lambda to: z_copy(c, to, z).start())
+        z_own(c).start()
+
+    def start_p(c):
+        each_place(lambda py, px: p_copy(c, py, px, place).start())
+        p_own(c).start()
+
+    def wait_z(c):
+        z_own(c).wait()
+        each_z(lambda to: z_copy(c, to, to).wait_recv())
+
+    def wait_p(c):
+        p_own(c).wait()
+        each_place(lambda py, px: p_copy(c, py, px, py * NX + px).wait_recv())
 
     def wave_z(to, owner):
         return remote(
@@ -135,6 +163,7 @@
     each_z(lambda to: wave_z(to, z).start())
     wave_z_own.start()
 
+    first_order = (0, 3, 1, 4, 2)
     index = lax.broadcasted_iota(jnp.int32, (1, degrees), 1)
 
     def sums_of(slot):
@@ -149,7 +178,7 @@
         )
         return jnp.dot(both, legendre[slot], preferred_element_type=jnp.float32)
 
-    def synthesize(c, carry):
+    def synthesize(c):
         first = sums_of(2 * c)
         second = sums_of(2 * c + 1)
         for side in range(2):
@@ -160,11 +189,13 @@
                 send[c, d // (NZ * NX), (d // NX) % NZ, d % NX] = staged[
                     side, rows * slab:rows * slab + 8, :
                 ]
-        each_z(lambda to: z_copy(c, to, z).start())
-        z_own(c).start()
-        return carry
-
-    lax.fori_loop(0, chunks, synthesize, 0)
+
+    for c in first_order:
+        synthesize(c)
+        if c < line_first:
+            start_z(c)
+        else:
+            start_p(c)
 
     wave_z_own.wait()
     each_z(lambda to: wave_z(to, to).wait_recv())
@@ -206,15 +237,7 @@
     south = me // (OWNERS // 2)
     flat = recv.reshape(chunks * OWNERS * 8, LANES)
 
-    def forward(c):
-        z_own(c).wait()
-        each_z(lambda to: z_copy(c, to, to).wait_recv())
-        each_place(lambda py, px: p_copy(c, py, px, place).start())
-        p_own(c).start()
-
     def add_chunk(c):
-        p_own(c).wait()
-        each_place(lambda py, px: p_copy(c, py, px, py * NX + px).wait_recv())
         parts = [[], []]
         for row in range(rows):
             source = row + south * (rows - 1 - 2 * row)
@@ -237,18 +260,22 @@
             sums += jnp.dot(top, low[at, :], preferred_element_type=jnp.float32)
             total[...] += sums
 
-    forward(0)
+    wait_z(0)
+    start_p(0)
     lax.fori_loop(0, wave_rows.shape[0] // 16, fill, 0)
-
-    def later(c, carry):
-        @pl.when(c < chunks)
-        def _():
-            forward(c)
-
+    for c in range(1, line_first):
+        wait_z(c)
+        start_p(c)
+        if line_first - 1 + c < chunks:
+            wait_p(line_first - 1 + c)
+            start_z(line_first - 1 + c)
+        wait_p(c - 1)
         add_chunk(c - 1)
-        return carry
-
-    lax.fori_loop(1, chunks + 1, later, 0)
+    wait_p(line_first - 1)
+    add_chunk(line_first - 1)
+    for c in range(line_first, chunks):
+        wait_z(c)
+        add_chunk(c)
 
     r = lax.broadcasted_iota(jnp.int32, (TILE, TILE), 0)
     q = lax.broadcasted_iota(jnp.int32, (TILE, TILE), 1)
@@ -272,12 +299,9 @@
     each_z(lambda to: wave_z(to, z).wait_send())
     each_place(lambda py, px: wave_p(py, px, place).wait_send())
 
-    def drain(c, carry):
+    for c in range(chunks):
         each_z(lambda to: z_copy(c, to, z).wait_send())
         each_place(lambda py, px: p_copy(c, py, px, place).wait_send())
-        return carry
-
-    lax.fori_loop(0, chunks, drain, 0)
 
 
 def on_device(spectral, legendre, wavenumber):
@@ -285,12 +309,13 @@
     north = legendre.shape[2]
     rows = 2 * north // OWNERS
     chunks = slots // 2
+    line_first = 3
     coeff = jnp.transpose(spectral, (0, 2, 3, 1)).reshape(slots, 2 * levels, degrees)
     depth = slots * OWNERS
     half = NLON // 2
     f32, bf16, i32 = jnp.float32, jnp.bfloat16, jnp.int32
     grid = pl.pallas_call(
-        functools.partial(transform_kernel, chunks, rows),
+        functools.partial(transform_kernel, chunks, line_first, rows),
         out_shape=jax.ShapeDtypeStruct((rows, levels, NLON), f32),
         in_specs=[
             pl.BlockSpec(memory_space=pltpu.SMEM),
@@ -303,7 +328,8 @@
             pltpu.VMEM((slots, degrees, north), bf16),
             pltpu.VMEM((2, north + 8, LANES), f32),
             pltpu.VMEM((chunks, NY, NZ, NX, 8, LANES), f32),
-            pltpu.VMEM((chunks, NZ, NY, NX, 8, LANES), f32),
+            pltpu.VMEM((line_first, NZ, NY, NX, 8, LANES), f32),
+            pltpu.VMEM((chunks - line_first, PLANE, NZ, 8, LANES), f32),
             pltpu.VMEM((chunks, PLANE, NZ, 8, LANES), f32),
             pltpu.VMEM((8, LANES), i32),
             pltpu.VMEM((NZ, 8, LANES), i32),

time: 73.3 us -> 64.3 us (0.88)
  Pallas kernels: 70.2 us -> 61.2 us
    pallas_call x1, Pallas kernels: 70.2 us -> 61.2 us  [on_device(): pl.pallas_call(functools.partial(transform_kernel, chunks, line_first, ro...]
where the time goes in v1:
time: 64.3 us; the launch traced here: 64.2 us
  Pallas kernels  61.2 us (95%)
  local copies, waits for them, and re-layouts  2.99 us (5%)
    pallas_call x1, Pallas kernels, on_device(): pl.pallas_call(functools.partial(transform_kernel, chunks, line_first, ro...  61.2 us
    unnamed x1, local copies, waits for them, and re-layouts  2.99 us

profile of v1, /device:TPU:1, one launch (start us, length us, event | category | flops | bytes accessed | tf_op | source)
XLA Modules:
  0.0 64.2 jit_solution(3275798962477825273)
XLA Ops:
  0.0 61.2 %shard_map.37 = f32[6,32,2560]{2,1,0:T(8,128)} custom-call(s32[10]{0:T(128)} %wave_smem.1, bf16[10,64,1280]{2,1,0:T(8,128)(2,1)} %bitcast.5, bf16[10,1280,384]{2,1,0:T(8,128)(2,1)} %legendre_hbm.1), custom_call_target="tpu_custom_call" | custom-call | tf_op jit(solution)/shard_map/pallas_call | solution.py:317
  61.2 3.0 %copy.5 = f32[6,2560,32]{1,2,0:T(8,128)} copy(f32[6,2560,32]{1,2,0:T(8,128)} %bitcast.4) | data formatting | bytes 3932160

commit v2 on v1

--- a/solution.py
+++ b/solution.py
@@ -140,9 +140,13 @@
             pltpu.make_async_copy(legendre_hbm.at[slot], legendre.at[slot], load_sem.at[1, slot]),
         )
 
-    for slot in range(slots):
-        for copy in load(slot):
-            copy.start()
+    def start_load(c):
+        for slot in (2 * c, 2 * c + 1):
+            for copy in load(slot):
+                copy.start()
+
+    first_order = (0, 3, 1, 4, 2)
+    start_load(first_order[0])
 
     barrier = pltpu.get_barrier_semaphore()
 
@@ -159,16 +163,10 @@
         waves = jnp.where(at_slot == slot, wave_smem[slot], waves)
     wave_row[...] = waves
     staged[...] = jnp.zeros(staged.shape, jnp.float32)
-    pl.semaphore_wait(barrier, NZ - 1 + PLANE - 1)
-    each_z(lambda to: wave_z(to, z).start())
-    wave_z_own.start()
-
-    first_order = (0, 3, 1, 4, 2)
+
     index = lax.broadcasted_iota(jnp.int32, (1, degrees), 1)
 
     def sums_of(slot):
-        for copy in load(slot):
-            copy.wait()
         offset = index - wave_smem[slot]
         keep = jnp.where(offset >= 0, 1.0, 0.0)
         flip = jnp.where((offset & 1) == 0, keep, -keep)
@@ -191,7 +189,17 @@
                 ]
 
     for c in first_order:
+        for slot in (2 * c, 2 * c + 1):
+            for copy in load(slot):
+                copy.wait()
+        if c == first_order[0]:
+            for other in first_order[1:]:
+                start_load(other)
         synthesize(c)
+        if c == first_order[0]:
+            pl.semaphore_wait(barrier, NZ - 1 + PLANE - 1)
+            each_z(lambda to: wave_z(to, z).start())
+            wave_z_own.start()
         if c < line_first:
             start_z(c)
         else:
@@ -316,7 +324,7 @@
     f32, bf16, i32 = jnp.float32, jnp.bfloat16, jnp.int32
     grid = pl.pallas_call(
         functools.partial(transform_kernel, chunks, line_first, rows),
-        out_shape=jax.ShapeDtypeStruct((rows, levels, NLON), f32),
+        out_shape=pltpu.VMEM((rows, levels, NLON), f32),
         in_specs=[
             pl.BlockSpec(memory_space=pltpu.SMEM),
             pl.BlockSpec(memory_space=pltpu.HBM),
@@ -349,7 +357,7 @@
             pltpu.SemaphoreType.DMA((2, chunks + 1)),
         ],
         compiler_params=pltpu.CompilerParams(
-            collective_id=0, has_side_effects=True, vmem_limit_bytes=60 * 2**20,
+            collective_id=0, has_side_effects=True, vmem_limit_bytes=56 * 2**20,
         ),
     )(wavenumber, coeff, legendre)
     return jnp.transpose(grid, (0, 2, 1))

time: 64.3 us -> 60.1 us (0.935)
  Pallas kernels: 61.2 us -> 58.4 us
  local copies, waits for them, and re-layouts: 2.99 us -> 1.27 us
    pallas_call x1, Pallas kernels: 61.2 us -> 58.4 us  [on_device(): pl.pallas_call(functools.partial(transform_kernel, chunks, line_first, ro...]
    unnamed x1, local copies, waits for them, and re-layouts: 2.99 us -> 1.27 us
where the time goes in v2:
time: 60.1 us; the launch traced here: 59.7 us
  Pallas kernels  58.4 us (97%)
  local copies, waits for them, and re-layouts  1.27 us (2%)
    pallas_call x1, Pallas kernels, on_device(): pl.pallas_call(functools.partial(transform_kernel, chunks, line_first, ro...  58.4 us
    unnamed x1, local copies, waits for them, and re-layouts  1.27 us

profile of v2, /device:TPU:1, one launch (start us, length us, event | category | flops | bytes accessed | tf_op | source)
XLA Modules:
  0.0 59.7 jit_solution(3193382019467960010)
XLA Ops:
  0.0 58.4 %shard_map.37 = f32[6,32,2560]{2,1,0:T(8,128)S(1)} custom-call(s32[10]{0:T(128)} %wave_smem.1, bf16[10,64,1280]{2,1,0:T(8,128)(2,1)} %bitcast.5, bf16[10,1280,384]{2,1,0:T(8,128)(2,1)} %legendre_hbm.1), custom_call_target="tpu_custom_call" | custom-call | tf_op jit(solution)/shard_map/pallas_call | solution.py:325
  58.4 1.3 %copy.5 = f32[6,2560,32]{1,2,0:T(8,128)} copy(f32[6,2560,32]{1,2,0:T(8,128)S(1)} %bitcast.4) | data formatting | bytes 3932160

commit v3 on v2

--- a/solution.py
+++ b/solution.py
@@ -32,7 +32,7 @@
 
 
 def transform_kernel(
-    chunks, line_first, rows,
+    chunks, line_first, groups, rows,
     wave_smem, spectral_hbm, legendre_hbm,
     out,
     spectral, legendre, staged, send, middle, spread, recv,
@@ -64,21 +64,37 @@
         for d in (5, 15, 7, 13, 10, 6, 9, 14, 11, 2, 8, 1, 4, 3, 12):
             act((y + d // NX) % NY, (x + d % NX) % NX)
 
-    def z_copy(c, to, owner):
-        if c < line_first:
-            src, dst = send.at[c, :, to, :, 0:rows, :], middle.at[c, owner, :, :, 0:rows, :]
+    def z_views(c, g, to, owner):
+        if c < line_first:
+            return send.at[c, :, to, :, 0:rows, :], middle.at[c, owner, :, :, 0:rows, :]
+        part = slice(g * rows // groups, (g + 1) * rows // groups) if c == chunks - 1 else slice(0, rows)
+        return spread.at[c - line_first, :, to, part, :], recv.at[c, :, owner, part, :]
+
+    def z_copy(c, g, to, owner):
+        src, dst = z_views(c, g, to, owner)
+        return remote(src, dst, z_send.at[c + g], z_recv.at[c + g], peer_at(y, to, x))
+
+    def z_own(c, g):
+        src, dst = z_views(c, g, z, z)
+        return pltpu.make_async_copy(src, dst, own_sem.at[0, c + g])
+
+    def z_all(c, g):
+        if c < line_first:
+            landed = middle.at[c, 0:NZ - 1, :, :, 0:rows, :]
         else:
-            src = spread.at[c - line_first, :, to, 0:rows, :]
-            dst = recv.at[c, :, owner, 0:rows, :]
-        return remote(src, dst, z_send.at[c, to], z_recv.at[c, owner], peer_at(y, to, x))
-
-    def z_own(c):
-        if c < line_first:
-            src, dst = send.at[c, :, z, :, 0:rows, :], middle.at[c, z, :, :, 0:rows, :]
+            part = slice(g * rows // groups, (g + 1) * rows // groups) if c == chunks - 1 else slice(0, rows)
+            landed = recv.at[c, :, 0:NZ - 1, part, :]
+        return remote(landed, landed, z_send.at[c + g], z_recv.at[c + g], peer_at(y, (z + 1) % NZ, x))
+
+    def p_all(c):
+        if c < line_first:
+            landed = recv.at[c, 0:PLANE - 1, :, 0:rows, :]
         else:
-            src = spread.at[c - line_first, :, z, 0:rows, :]
-            dst = recv.at[c, :, z, 0:rows, :]
-        return pltpu.make_async_copy(src, dst, own_sem.at[0, c])
+            landed = spread.at[c - line_first, 0:PLANE - 1, :, 0:rows, :]
+        return remote(landed, landed, p_send.at[c], p_recv.at[c], peer_at(y, z, (x + 1) % NX))
+
+    def groups_of(c):
+        return range(groups if c == chunks - 1 else 1)
 
     def p_copy(c, py, px, owner):
         if c < line_first:
@@ -87,7 +103,7 @@
             src = send.at[c, py, :, px, 0:rows, :]
             dst = spread.at[c - line_first, owner, :, 0:rows, :]
         return remote(
-            src, dst, p_send.at[c, py * NX + px], p_recv.at[c, owner], peer_at(py, z, px)
+            src, dst, p_send.at[c], p_recv.at[c], peer_at(py, z, px)
         )
 
     def p_own(c):
@@ -99,51 +115,62 @@
         return pltpu.make_async_copy(src, dst, own_sem.at[1, c])
 
     def start_z(c):
-        each_z(lambda to: z_copy(c, to, z).start())
-        z_own(c).start()
+        for g in groups_of(c):
+            each_z(lambda to: z_copy(c, g, to, z).start())
+            z_own(c, g).start()
 
     def start_p(c):
         each_place(lambda py, px: p_copy(c, py, px, place).start())
         p_own(c).start()
 
-    def wait_z(c):
-        z_own(c).wait()
-        each_z(lambda to: z_copy(c, to, to).wait_recv())
+    def wait_z(c, g=0):
+        z_own(c, g).wait()
+        z_all(c, g).wait_recv()
 
     def wait_p(c):
         p_own(c).wait()
-        each_place(lambda py, px: p_copy(c, py, px, py * NX + px).wait_recv())
+        p_all(c).wait_recv()
+
+    wave_job = chunks - 1 + groups
 
     def wave_z(to, owner):
         return remote(
             wave_row.at[0:1, :], wave_mid.at[owner, 0:1, :],
-            z_send.at[chunks, to], z_recv.at[chunks, owner], peer_at(y, to, x),
+            z_send.at[wave_job], z_recv.at[wave_job], peer_at(y, to, x),
         )
 
     wave_z_own = pltpu.make_async_copy(
-        wave_row.at[0:1, :], wave_mid.at[z, 0:1, :], own_sem.at[0, chunks]
+        wave_row.at[0:1, :], wave_mid.at[z, 0:1, :], own_sem.at[0, wave_job]
     )
 
     def wave_p(py, px, owner):
         return remote(
             wave_mid.at[:, 0:1, :], wave_all.at[owner, :, 0:1, :],
-            p_send.at[chunks, py * NX + px], p_recv.at[chunks, owner], peer_at(py, z, px),
-        )
-
+            p_send.at[chunks], p_recv.at[chunks], peer_at(py, z, px),
+        )
+
+    wave_z_all = remote(
+        wave_mid.at[0:NZ - 1, 0:1, :], wave_mid.at[0:NZ - 1, 0:1, :],
+        z_send.at[wave_job], z_recv.at[wave_job], peer_at(y, (z + 1) % NZ, x),
+    )
+    wave_p_all = remote(
+        wave_all.at[0:PLANE - 1, :, 0:1, :], wave_all.at[0:PLANE - 1, :, 0:1, :],
+        p_send.at[chunks], p_recv.at[chunks], peer_at(y, z, (x + 1) % NX),
+    )
     wave_p_own = pltpu.make_async_copy(
         wave_mid.at[:, 0:1, :], wave_all.at[place, :, 0:1, :], own_sem.at[1, chunks]
     )
 
-    def load(slot):
+    def load(c):
+        pair = slice(2 * c, 2 * c + 2)
         return (
-            pltpu.make_async_copy(spectral_hbm.at[slot], spectral.at[slot], load_sem.at[0, slot]),
-            pltpu.make_async_copy(legendre_hbm.at[slot], legendre.at[slot], load_sem.at[1, slot]),
+            pltpu.make_async_copy(spectral_hbm.at[pair], spectral.at[pair], load_sem.at[0, c]),
+            pltpu.make_async_copy(legendre_hbm.at[pair], legendre.at[pair], load_sem.at[1, c]),
         )
 
     def start_load(c):
-        for slot in (2 * c, 2 * c + 1):
-            for copy in load(slot):
-                copy.start()
+        for copy in load(c):
+            copy.start()
 
     first_order = (0, 3, 1, 4, 2)
     start_load(first_order[0])
@@ -189,9 +216,8 @@
                 ]
 
     for c in first_order:
-        for slot in (2 * c, 2 * c + 1):
-            for copy in load(slot):
-                copy.wait()
+        for copy in load(c):
+            copy.wait()
         if c == first_order[0]:
             for other in first_order[1:]:
                 start_load(other)
@@ -202,18 +228,27 @@
             wave_z_own.start()
         if c < line_first:
             start_z(c)
-        else:
-            start_p(c)
 
     wave_z_own.wait()
-    each_z(lambda to: wave_z(to, to).wait_recv())
+    wave_z_all.wait_recv()
     each_place(lambda py, px: wave_p(py, px, place).start())
     wave_p_own.start()
+    for c in range(line_first, chunks):
+        start_p(c)
     even[...] = jnp.zeros(even.shape, jnp.float32)
     odd[...] = jnp.zeros(odd.shape, jnp.float32)
 
+    def drain_z(c):
+        for g in groups_of(c):
+            z_all(c, g).wait_send()
+
+    def drain_p(c):
+        p_all(c).wait_send()
+
+    wait_z(0)
+    start_p(0)
     wave_p_own.wait()
-    each_place(lambda py, px: wave_p(py, px, py * NX + px).wait_recv())
+    wave_p_all.wait_recv()
     flat_waves = wave_all.reshape(OWNERS * 8, LANES)
     gathered = flat_waves[pl.ds(0, OWNERS, stride=8), :].astype(jnp.float32)
     for slot in range(slots):
@@ -245,11 +280,10 @@
     south = me // (OWNERS // 2)
     flat = recv.reshape(chunks * OWNERS * 8, LANES)
 
-    def add_chunk(c):
+    def add_chunk(c, low_row=0, high_row=rows):
         parts = [[], []]
-        for row in range(rows):
-            source = row + south * (rows - 1 - 2 * row)
-            turned = flat[pl.ds(c * OWNERS * 8 + source, OWNERS, stride=8), :].T
+        for row in range(low_row, high_row):
+            turned = flat[pl.ds(c * OWNERS * 8 + row, OWNERS, stride=8), :].T
             for part in range(2):
                 parts[part].append(
                     jnp.concatenate(
@@ -266,12 +300,16 @@
             sums = jnp.dot(top, table, preferred_element_type=jnp.float32)
             sums += jnp.dot(rest, table, preferred_element_type=jnp.float32)
             sums += jnp.dot(top, low[at, :], preferred_element_type=jnp.float32)
-            total[...] += sums
-
-    wait_z(0)
-    start_p(0)
+            total[low_row * levels:high_row * levels, :] += sums
+
     lax.fori_loop(0, wave_rows.shape[0] // 16, fill, 0)
     for c in range(1, line_first):
+        if c == line_first - 1:
+            wave_z_all.wait_send()
+            wave_p_all.wait_send()
+            drain_z(0)
+            drain_p(line_first)
+            drain_p(line_first + 1)
         wait_z(c)
         start_p(c)
         if line_first - 1 + c < chunks:
@@ -281,7 +319,7 @@
         add_chunk(c - 1)
     wait_p(line_first - 1)
     add_chunk(line_first - 1)
-    for c in range(line_first, chunks):
+    for c in range(line_first, chunks - 1):
         wait_z(c)
         add_chunk(c)
 
@@ -290,26 +328,40 @@
     mirror = jnp.where(r + q == TILE, 1.0, 0.0).astype(jnp.bfloat16)
     at_zero = lax.broadcasted_iota(jnp.int32, (1, TILE), 1) == 0
     tiles = odd.shape[1] // TILE
-    after = even[:, tiles * TILE:tiles * TILE + 1]
-    for tile in range(tiles - 1, -1, -1):
-        to = slice(tile * TILE, (tile + 1) * TILE)
-        back = slice((2 * tiles - 1 - tile) * TILE, (2 * tiles - tile) * TILE)
-        e, o = even[:, to], odd[:, to]
-        out[:, :, to] = (e - o).reshape(rows, levels, TILE)
-        d = e + o
-        top = d.astype(jnp.bfloat16)
-        rest = (d - top.astype(jnp.float32)).astype(jnp.bfloat16)
-        turned = jnp.dot(top, mirror, preferred_element_type=jnp.float32)
-        turned += jnp.dot(rest, mirror, preferred_element_type=jnp.float32)
-        out[:, :, back] = jnp.where(at_zero, after, turned).reshape(rows, levels, TILE)
-        after = d[:, 0:1]
-
-    each_z(lambda to: wave_z(to, z).wait_send())
-    each_place(lambda py, px: wave_p(py, px, place).wait_send())
-
-    for c in range(chunks):
-        each_z(lambda to: z_copy(c, to, z).wait_send())
-        each_place(lambda py, px: p_copy(c, py, px, place).wait_send())
+
+    def finish(low_row, high_row):
+        at = slice(low_row * levels, high_row * levels)
+
+        def put(values, to):
+            for row in range(low_row, high_row):
+                target = row + south * (rows - 1 - 2 * row)
+                out[target, :, to] = values[(row - low_row) * levels:(row - low_row + 1) * levels]
+
+        after = even[at, tiles * TILE:tiles * TILE + 1]
+        for tile in range(tiles - 1, -1, -1):
+            to = slice(tile * TILE, (tile + 1) * TILE)
+            back = slice((2 * tiles - 1 - tile) * TILE, (2 * tiles - tile) * TILE)
+            e, o = even[at, to], odd[at, to]
+            put(e - o, to)
+            d = e + o
+            top = d.astype(jnp.bfloat16)
+            rest = (d - top.astype(jnp.float32)).astype(jnp.bfloat16)
+            turned = jnp.dot(top, mirror, preferred_element_type=jnp.float32)
+            turned += jnp.dot(rest, mirror, preferred_element_type=jnp.float32)
+            put(jnp.where(at_zero, after, turned), back)
+            after = d[:, 0:1]
+
+    for c in range(1, chunks - 1):
+        drain_z(c)
+    for c in range(line_first):
+        drain_p(c)
+    for g in range(groups):
+        wait_z(chunks - 1, g)
+        low_row, high_row = g * rows // groups, (g + 1) * rows // groups
+        add_chunk(chunks - 1, low_row, high_row)
+        finish(low_row, high_row)
+
+    drain_z(chunks - 1)
 
 
 def on_device(spectral, legendre, wavenumber):
@@ -318,12 +370,13 @@
     rows = 2 * north // OWNERS
     chunks = slots // 2
     line_first = 3
+    groups = 2
     coeff = jnp.transpose(spectral, (0, 2, 3, 1)).reshape(slots, 2 * levels, degrees)
     depth = slots * OWNERS
     half = NLON // 2
     f32, bf16, i32 = jnp.float32, jnp.bfloat16, jnp.int32
     grid = pl.pallas_call(
-        functools.partial(transform_kernel, chunks, line_first, rows),
+        functools.partial(transform_kernel, chunks, line_first, groups, rows),
         out_shape=pltpu.VMEM((rows, levels, NLON), f32),
         in_specs=[
             pl.BlockSpec(memory_space=pltpu.SMEM),
@@ -349,12 +402,12 @@
             pltpu.VMEM((depth, half), bf16),
             pltpu.VMEM((rows * levels, half + LANES), f32),
             pltpu.VMEM((rows * levels, half), f32),
-            pltpu.SemaphoreType.DMA((2, slots)),
-            pltpu.SemaphoreType.DMA((chunks + 1, NZ)),
-            pltpu.SemaphoreType.DMA((chunks + 1, NZ)),
-            pltpu.SemaphoreType.DMA((chunks + 1, PLANE)),
-            pltpu.SemaphoreType.DMA((chunks + 1, PLANE)),
-            pltpu.SemaphoreType.DMA((2, chunks + 1)),
+            pltpu.SemaphoreType.DMA((2, chunks)),
+            pltpu.SemaphoreType.DMA((chunks + groups,)),
+            pltpu.SemaphoreType.DMA((chunks + groups,)),
+            pltpu.SemaphoreType.DMA((chunks + 1,)),
+            pltpu.SemaphoreType.DMA((chunks + 1,)),
+            pltpu.SemaphoreType.DMA((2, chunks + groups)),
         ],
         compiler_params=pltpu.CompilerParams(
             collective_id=0, has_side_effects=True, vmem_limit_bytes=56 * 2**20,

time: 60.1 us -> 57.7 us (0.960)
  Pallas kernels: 58.4 us -> 56.1 us
    pallas_call x1, Pallas kernels: 58.4 us -> 56.1 us  [on_device(): pl.pallas_call(functools.partial(transform_kernel, chunks, line_first, gr...]
where the time goes in v3:
time: 57.7 us; the launch traced here: 57.4 us
  Pallas kernels  56.1 us (97%)
  local copies, waits for them, and re-layouts  1.27 us (2%)
    pallas_call x1, Pallas kernels, on_device(): pl.pallas_call(functools.partial(transform_kernel, chunks, line_first, gr...  56.1 us
    unnamed x1, local copies, waits for them, and re-layouts  1.27 us

profile of v3, /device:TPU:1, one launch (start us, length us, event | category | flops | bytes accessed | tf_op | source)
XLA Modules:
  0.0 57.4 jit_solution(18399588454809371684)
XLA Ops:
  0.0 56.1 %shard_map.37 = f32[6,32,2560]{2,1,0:T(8,128)S(1)} custom-call(s32[10]{0:T(128)} %wave_smem.1, bf16[10,64,1280]{2,1,0:T(8,128)(2,1)} %bitcast.5, bf16[10,1280,384]{2,1,0:T(8,128)(2,1)} %legendre_hbm.1), custom_call_target="tpu_custom_call" | custom-call | tf_op jit(solution)/shard_map/pallas_call | solution.py:378
  56.1 1.3 %copy.5 = f32[6,2560,32]{1,2,0:T(8,128)} copy(f32[6,2560,32]{1,2,0:T(8,128)S(1)} %bitcast.4) | data formatting | bytes 3932160

commit v4 on v3

--- a/solution.py
+++ b/solution.py
@@ -33,12 +33,12 @@
 
 def transform_kernel(
     chunks, line_first, groups, rows,
-    wave_smem, spectral_hbm, legendre_hbm,
+    wave_hbm, spectral_hbm, legendre_hbm,
     out,
-    spectral, legendre, staged, send, middle, spread, recv,
+    wave_smem, spectral, legendre, staged, send, middle, spread, recv,
     wave_row, wave_mid, wave_all, wave_rows,
     cos_hi, cos_lo, sin_hi, sin_lo, even, odd,
-    load_sem, z_send, z_recv, p_send, p_recv, own_sem,
+    load_sem, z_send, z_recv, p_send, p_recv, own_sem, wave_sem,
 ):
     me = lax.axis_index("wa")
     y, z, x = me // (NZ * NX), (me // NX) % NZ, me % NX
@@ -173,6 +173,8 @@
             copy.start()
 
     first_order = (0, 3, 1, 4, 2)
+    own_waves = pltpu.make_async_copy(wave_hbm, wave_smem, wave_sem)
+    own_waves.start()
     start_load(first_order[0])
 
     barrier = pltpu.get_barrier_semaphore()
@@ -184,6 +186,7 @@
 
     each_z(lambda to: greet(peer_at(y, to, x)))
     each_place(lambda py, px: greet(peer_at(py, z, px)))
+    own_waves.wait()
     at_slot = lax.broadcasted_iota(jnp.int32, wave_row.shape, 1)
     waves = jnp.zeros(wave_row.shape, jnp.int32)
     for slot in range(slots):
@@ -379,12 +382,13 @@
         functools.partial(transform_kernel, chunks, line_first, groups, rows),
         out_shape=pltpu.VMEM((rows, levels, NLON), f32),
         in_specs=[
-            pl.BlockSpec(memory_space=pltpu.SMEM),
+            pl.BlockSpec(memory_space=pltpu.HBM),
             pl.BlockSpec(memory_space=pltpu.HBM),
             pl.BlockSpec(memory_space=pltpu.HBM),
         ],
         out_specs=pl.BlockSpec(memory_space=pltpu.VMEM),
         scratch_shapes=[
+            pltpu.SMEM((slots,), i32),
             pltpu.VMEM((slots, 2 * levels, degrees), bf16),
             pltpu.VMEM((slots, degrees, north), bf16),
             pltpu.VMEM((2, north + 8, LANES), f32),
@@ -408,6 +412,7 @@
             pltpu.SemaphoreType.DMA((chunks + 1,)),
             pltpu.SemaphoreType.DMA((chunks + 1,)),
             pltpu.SemaphoreType.DMA((2, chunks + groups)),
+            pltpu.SemaphoreType.DMA,
         ],
         compiler_params=pltpu.CompilerParams(
             collective_id=0, has_side_effects=True, vmem_limit_bytes=56 * 2**20,

time: 57.7 us -> 56.7 us (0.983)
  Pallas kernels: 56.1 us -> 55.3 us
    pallas_call x1, Pallas kernels: 56.1 us -> 55.3 us  [on_device(): pl.pallas_call(functools.partial(transform_kernel, chunks, line_first, gr...]
where the time goes in v4:
time: 56.7 us; the launch traced here: 56.6 us
  Pallas kernels  55.3 us (98%)
  local copies, waits for them, and re-layouts  1.27 us (2%)
    pallas_call x1, Pallas kernels, on_device(): pl.pallas_call(functools.partial(transform_kernel, chunks, line_first, gr...  55.3 us
    unnamed x1, local copies, waits for them, and re-layouts  1.27 us

profile of v4, /device:TPU:1, one launch (start us, length us, event | category | flops | bytes accessed | tf_op | source)
XLA Modules:
  0.0 56.6 jit_solution(2233296337912973730)
XLA Ops:
  0.0 55.3 %shard_map.37 = f32[6,32,2560]{2,1,0:T(8,128)S(1)} custom-call(s32[10]{0:T(128)} %wave_hbm.1, bf16[10,64,1280]{2,1,0:T(8,128)(2,1)} %bitcast.5, bf16[10,1280,384]{2,1,0:T(8,128)(2,1)} %legendre_hbm.1), custom_call_target="tpu_custom_call" | custom-call | tf_op jit(solution)/shard_map/pallas_call | solution.py:381
  55.3 1.3 %copy.5 = f32[6,2560,32]{1,2,0:T(8,128)} copy(f32[6,2560,32]{1,2,0:T(8,128)S(1)} %bitcast.4) | data formatting | bytes 3932160

commit v5 on v4

--- a/solution.py
+++ b/solution.py
@@ -76,21 +76,21 @@
 
     def z_own(c, g):
         src, dst = z_views(c, g, z, z)
-        return pltpu.make_async_copy(src, dst, own_sem.at[0, c + g])
-
-    def z_all(c, g):
-        if c < line_first:
-            landed = middle.at[c, 0:NZ - 1, :, :, 0:rows, :]
+        return pltpu.make_async_copy(src, dst, z_recv.at[c + g])
+
+    def z_all(c, g, owners):
+        if c < line_first:
+            landed = middle.at[c, 0:owners, :, :, 0:rows, :]
         else:
             part = slice(g * rows // groups, (g + 1) * rows // groups) if c == chunks - 1 else slice(0, rows)
-            landed = recv.at[c, :, 0:NZ - 1, part, :]
+            landed = recv.at[c, :, 0:owners, part, :]
         return remote(landed, landed, z_send.at[c + g], z_recv.at[c + g], peer_at(y, (z + 1) % NZ, x))
 
-    def p_all(c):
-        if c < line_first:
-            landed = recv.at[c, 0:PLANE - 1, :, 0:rows, :]
+    def p_all(c, owners):
+        if c < line_first:
+            landed = recv.at[c, 0:owners, :, 0:rows, :]
         else:
-            landed = spread.at[c - line_first, 0:PLANE - 1, :, 0:rows, :]
+            landed = spread.at[c - line_first, 0:owners, :, 0:rows, :]
         return remote(landed, landed, p_send.at[c], p_recv.at[c], peer_at(y, z, (x + 1) % NX))
 
     def groups_of(c):
@@ -112,7 +112,7 @@
         else:
             src = send.at[c, y, :, x, 0:rows, :]
             dst = spread.at[c - line_first, place, :, 0:rows, :]
-        return pltpu.make_async_copy(src, dst, own_sem.at[1, c])
+        return pltpu.make_async_copy(src, dst, p_recv.at[c])
 
     def start_z(c):
         for g in groups_of(c):
@@ -124,12 +124,10 @@
         p_own(c).start()
 
     def wait_z(c, g=0):
-        z_own(c, g).wait()
-        z_all(c, g).wait_recv()
+        z_all(c, g, NZ).wait_recv()
 
     def wait_p(c):
-        p_own(c).wait()
-        p_all(c).wait_recv()
+        p_all(c, PLANE).wait_recv()
 
     wave_job = chunks - 1 + groups
 
@@ -140,7 +138,7 @@
         )
 
     wave_z_own = pltpu.make_async_copy(
-        wave_row.at[0:1, :], wave_mid.at[z, 0:1, :], own_sem.at[0, wave_job]
+        wave_row.at[0:1, :], wave_mid.at[z, 0:1, :], own_sem.at[0]
     )
 
     def wave_p(py, px, owner):
@@ -158,14 +156,14 @@
         p_send.at[chunks], p_recv.at[chunks], peer_at(y, z, (x + 1) % NX),
     )
     wave_p_own = pltpu.make_async_copy(
-        wave_mid.at[:, 0:1, :], wave_all.at[place, :, 0:1, :], own_sem.at[1, chunks]
+        wave_mid.at[:, 0:1, :], wave_all.at[place, :, 0:1, :], own_sem.at[1]
     )
 
     def load(c):
         pair = slice(2 * c, 2 * c + 2)
         return (
+            pltpu.make_async_copy(legendre_hbm.at[pair], legendre.at[pair], load_sem.at[1, c]),
             pltpu.make_async_copy(spectral_hbm.at[pair], spectral.at[pair], load_sem.at[0, c]),
-            pltpu.make_async_copy(legendre_hbm.at[pair], legendre.at[pair], load_sem.at[1, c]),
         )
 
     def start_load(c):
@@ -238,15 +236,13 @@
     wave_p_own.start()
     for c in range(line_first, chunks):
         start_p(c)
-    even[...] = jnp.zeros(even.shape, jnp.float32)
-    odd[...] = jnp.zeros(odd.shape, jnp.float32)
 
     def drain_z(c):
         for g in groups_of(c):
-            z_all(c, g).wait_send()
+            z_all(c, g, NZ - 1).wait_send()
 
     def drain_p(c):
-        p_all(c).wait_send()
+        p_all(c, PLANE - 1).wait_send()
 
     wait_z(0)
     start_p(0)
@@ -303,7 +299,10 @@
             sums = jnp.dot(top, table, preferred_element_type=jnp.float32)
             sums += jnp.dot(rest, table, preferred_element_type=jnp.float32)
             sums += jnp.dot(top, low[at, :], preferred_element_type=jnp.float32)
-            total[low_row * levels:high_row * levels, :] += sums
+            if c == 0:
+                total[...] = sums
+            else:
+                total[low_row * levels:high_row * levels, :] += sums
 
     lax.fori_loop(0, wave_rows.shape[0] // 16, fill, 0)
     for c in range(1, line_first):
@@ -411,7 +410,7 @@
             pltpu.SemaphoreType.DMA((chunks + groups,)),
             pltpu.SemaphoreType.DMA((chunks + 1,)),
             pltpu.SemaphoreType.DMA((chunks + 1,)),
-            pltpu.SemaphoreType.DMA((2, chunks + groups)),
+            pltpu.SemaphoreType.DMA((2,)),
             pltpu.SemaphoreType.DMA,
         ],
         compiler_params=pltpu.CompilerParams(

time: 56.7 us -> 56.7 us (level)
  no operation moved by 1% of the time
where the time goes in v5:
time: 56.7 us; the launch traced here: 56.5 us
  Pallas kernels  55.2 us (97%)
  local copies, waits for them, and re-layouts  1.27 us (2%)
    pallas_call x1, Pallas kernels, on_device(): pl.pallas_call(functools.partial(transform_kernel, chunks, line_first, gr...  55.2 us
    unnamed x1, local copies, waits for them, and re-layouts  1.27 us

profile of v5, /device:TPU:1, one launch (start us, length us, event | category | flops | bytes accessed | tf_op | source)
XLA Modules:
  0.0 56.5 jit_solution(1742879565943384919)
XLA Ops:
  0.0 55.2 %shard_map.37 = f32[6,32,2560]{2,1,0:T(8,128)S(1)} custom-call(s32[10]{0:T(128)} %wave_hbm.1, bf16[10,64,1280]{2,1,0:T(8,128)(2,1)} %bitcast.5, bf16[10,1280,384]{2,1,0:T(8,128)(2,1)} %legendre_hbm.1), custom_call_target="tpu_custom_call" | custom-call | tf_op jit(solution)/shard_map/pallas_call | solution.py:380
  55.2 1.3 %copy.5 = f32[6,2560,32]{1,2,0:T(8,128)} copy(f32[6,2560,32]{1,2,0:T(8,128)S(1)} %bitcast.4) | data formatting | bytes 3932160

commit v6 on v5

--- a/solution.py
+++ b/solution.py
@@ -170,7 +170,7 @@
         for copy in load(c):
             copy.start()
 
-    first_order = (0, 3, 1, 4, 2)
+    first_order = (0, 1, 2, 3, 4)
     own_waves = pltpu.make_async_copy(wave_hbm, wave_smem, wave_sem)
     own_waves.start()
     start_load(first_order[0])

time: 56.7 us -> 56.7 us (level)
  no operation moved by 1% of the time
where the time goes in v6:
time: 56.7 us; the launch traced here: 56.5 us
  Pallas kernels  55.2 us (97%)
  local copies, waits for them, and re-layouts  1.27 us (2%)
    pallas_call x1, Pallas kernels, on_device(): pl.pallas_call(functools.partial(transform_kernel, chunks, line_first, gr...  55.2 us
    unnamed x1, local copies, waits for them, and re-layouts  1.27 us

profile of v6, /device:TPU:1, one launch (start us, length us, event | category | flops | bytes accessed | tf_op | source)
XLA Modules:
  0.0 56.5 jit_solution(12904718793845573797)
XLA Ops:
  0.0 55.2 %shard_map.37 = f32[6,32,2560]{2,1,0:T(8,128)S(1)} custom-call(s32[10]{0:T(128)} %wave_hbm.1, bf16[10,64,1280]{2,1,0:T(8,128)(2,1)} %bitcast.5, bf16[10,1280,384]{2,1,0:T(8,128)(2,1)} %legendre_hbm.1), custom_call_target="tpu_custom_call" | custom-call | tf_op jit(solution)/shard_map/pallas_call | solution.py:380
  55.2 1.3 %copy.5 = f32[6,2560,32]{1,2,0:T(8,128)} copy(f32[6,2560,32]{1,2,0:T(8,128)S(1)} %bitcast.4) | data formatting | bytes 3932160
